TPU v7x, 32 devices: a whole 2x2x4 slice. The times are simulated.
32 devices in a mesh: region: 8 (over z, x), tm: 4 (over y, core).
Axes of the slice: x: 2, y: 2, z: 4, core: 2. Of those that a mesh axis runs over, the one named last changes fastest.
Arguments:
- observations: bfloat16 [8, 4, 2048, 512], P('region', 'tm'), may hold values from -160 to 160
- counts: int32 [8, 4], P('region', 'tm'), may hold values from 1 to 8, as said below
- visible: int32 [8, 8], replicated, may hold values 0 or 1
- latents: bfloat16 [8, 32, 512], P('region'), may hold values from -6 to 6
- lat_gain: float32 [512], replicated, may hold values from 0.5 to 1.5
- mlp_gain: float32 [512], replicated, may hold values from 0.5 to 1.5
- w_query: bfloat16 [512, 512], replicated, may hold values from -0.25 to 0.25
- w_keyval: bfloat16 [512, 1024], replicated, may hold values from -0.25 to 0.25
- w_out: bfloat16 [512, 512], replicated, may hold values from -0.25 to 0.25
- w_up: bfloat16 [512, 2048], P(None, 'tm'), may hold values from -0.25 to 0.25
- w_down: bfloat16 [2048, 512], P('tm'), may hold values from -0.125 to 0.125
Outputs:
- encoded: bfloat16 [8, 32, 512], P('region')
Inputs may be any that keep to these rules, and one draw needn't show every extreme that they name: `counts`: some region and time slot holds 8 blocks.
All inputs are finite; a program needn't handle non-finite values.
Results may differ from a plain program's by a relative error of at most 0.0055.
The roundings to bfloat16 on the way count: a program that leaves them out, or rounds other values in their place, can miss the bound.
Values may be sent and summed in bfloat16 or wider, within the bound.
A program may use at most 64 MiB of HBM per device.

v0:
```python
import math
import jax
import jax.numpy as jnp
from jax import lax
from jax.sharding import PartitionSpec as P

H = 8
BLK = 256
NEG = -1e30


def joined(x, axis, combine):
    everything = jax.tree.map(lambda part: lax.all_gather(part, axis), x)
    leading = jax.tree.map(lambda part: part[0], everything)

    def step(k, so_far):
        return combine(so_far, jax.tree.map(lambda part: part[k], everything))

    return lax.fori_loop(1, lax.axis_size(axis), step, leading)


def layer_norm(values, gain):
    average = jnp.mean(values, axis=-1, keepdims=True)
    centered = values - average
    variance = jnp.mean(centered * centered, axis=-1, keepdims=True)
    return centered * lax.rsqrt(variance + 1e-05) * gain


def expand(factor, model_width):
    return jnp.repeat(factor, model_width // factor.shape[-1], axis=-1)


def combine(first, second):
    first_num, first_den, first_peak = first
    second_num, second_den, second_peak = second
    highest = jnp.maximum(first_peak, second_peak)
    first_scale = jnp.exp(first_peak - highest)
    second_scale = jnp.exp(second_peak - highest)
    numerator = first_num * expand(first_scale, first_num.shape[-1]) + second_num * expand(
        second_scale, second_num.shape[-1]
    )
    return (numerator, first_den * first_scale + second_den * second_scale, highest)


def partials(query_rows, key_heads, value_heads, allowed, head_size):
    row_count = query_rows.shape[0]
    query_heads = query_rows.reshape(row_count, H, head_size)
    scores = jnp.einsum(
        "qhd,khd->hqk", query_heads, key_heads, preferred_element_type=jnp.float32
    ) * head_size ** (-0.5)
    scores = jnp.where(allowed[None], scores, NEG)
    peaks = jnp.max(scores, axis=-1)
    weights = jnp.where(allowed[None], jnp.exp(scores - peaks[..., None]), 0.0)
    denominator = jnp.sum(weights, axis=-1)
    numerator = jnp.einsum(
        "hqk,khd->qhd",
        weights.astype(jnp.bfloat16),
        value_heads,
        preferred_element_type=jnp.float32,
    )
    return (numerator.reshape(row_count, H * head_size), denominator.T, peaks.T)


def on_device(
    observations,
    counts,
    visible,
    latents,
    lat_gain,
    mlp_gain,
    w_query,
    w_keyval,
    w_out,
    w_up,
    w_down,
):
    regions = lax.axis_size("region")
    own_region = lax.axis_index("region")
    latent_rows = latents.shape[1]
    model_width = latents.shape[2]
    head_size = model_width // H
    observed = observations[0, 0]
    obs_rows = observed.shape[0]
    latent_state = latents[0].astype(jnp.float32)
    normed = layer_norm(latent_state, lat_gain).astype(jnp.bfloat16)
    own_queries = jnp.dot(normed, w_query, preferred_element_type=jnp.float32).astype(jnp.bfloat16)
    every_query = lax.all_gather(own_queries, "region", axis=0, tiled=True)
    keyval = jnp.dot(observed, w_keyval, preferred_element_type=jnp.float32).astype(jnp.bfloat16)
    key_heads = keyval[:, :model_width].reshape(obs_rows, H, head_size)
    value_heads = keyval[:, model_width:].reshape(obs_rows, H, head_size)
    live_rows = lax.iota(jnp.int32, obs_rows) < counts[0, 0] * BLK
    column = lax.dynamic_slice_in_dim(visible, own_region, 1, 1)[:, 0]
    sees_source = (column > 0) | (lax.iota(jnp.int32, regions) == own_region)
    per_block = math.gcd(regions, max(1, 256 // latent_rows))
    block_count = regions // per_block
    query_blocks = every_query.reshape(block_count, per_block * latent_rows, model_width)
    sees_blocks = jnp.repeat(sees_source, latent_rows).reshape(block_count, per_block * latent_rows)

    def one_block(operands):
        query_rows, sees_rows = operands
        allowed = sees_rows[:, None] & live_rows[None, :]
        return partials(query_rows, key_heads, value_heads, allowed, head_size)

    numerators, denominators, peaks = lax.map(one_block, (query_blocks, sees_blocks))
    numerators = numerators.reshape(regions, latent_rows, model_width)
    denominators = denominators.reshape(regions, latent_rows, H)
    peaks = peaks.reshape(regions, latent_rows, H)
    got_num, got_den, got_peak = (
        lax.all_to_all(numerators, "region", split_axis=0, concat_axis=0, tiled=True),
        lax.all_to_all(denominators, "region", split_axis=0, concat_axis=0, tiled=True),
        lax.all_to_all(peaks, "region", split_axis=0, concat_axis=0, tiled=True),
    )
    highest = jnp.max(got_peak, axis=0)
    factor = jnp.exp(got_peak - highest[None])
    numerator = jnp.sum(got_num * expand(factor, model_width), axis=0)
    denominator = jnp.sum(got_den * factor, axis=0)
    numerator, denominator, highest = joined((numerator, denominator, highest), "tm", combine)
    attended = (numerator / expand(denominator, model_width)).astype(jnp.bfloat16)
    residual = latent_state + jnp.dot(attended, w_out, preferred_element_type=jnp.float32)
    normed2 = layer_norm(residual, mlp_gain).astype(jnp.bfloat16)
    hidden = jax.nn.gelu(
        jnp.dot(normed2, w_up, preferred_element_type=jnp.float32), approximate=True
    ).astype(jnp.bfloat16)
    mlp_part = jnp.dot(hidden, w_down, preferred_element_type=jnp.float32)
    mlp_total = lax.psum(mlp_part, "tm")
    return (residual + mlp_total).astype(jnp.bfloat16)[None]


def solution(mesh):
    placed = (
        P("region", "tm", None, None),
        P("region", "tm"),
        P(),
        P("region", None, None),
        P(),
        P(),
        P(),
        P(),
        P(),
        P(None, "tm"),
        P("tm", None),
    )
    return jax.shard_map(
        on_device, mesh=mesh, in_specs=placed, out_specs=P("region", None, None), check_vma=False
    )
```

profile of v0, /device:TPU:0, one launch (start us, length us, event | category | flops | bytes accessed | tf_op | source)
XLA Modules:
  0.0 166.7 jit_solution(793247751511443457)
XLA Ops:
  6.5 1.0 fusion.44
  7.6 0.1 broadcast_in_dim.82
  7.6 0.1 and.27
  8.4 0.9 convert_reduce_fusion
  9.3 0.9 fusion.16
  10.2 1.3 convolution_convert_fusion.1
  11.5 32.6 %all_gather.19 = bf16[256,512]{1,0:T(8,128)(2,1)S(1)} all-gather(bf16[32,512]{1,0:T(8,128)(2,1)S(1)} %convolution_convert_fusion.1), channel_id=1, replica_groups=mesh['region'=8,'tm'=4] {'region'}, dimensions={0}, use_global_device_ids=true | all-gather | bytes 294912 | tf_op jit(solution)/shard_map/all_gather | solution.py:87
  44.1 0.1 copy.27
  44.3 3.6 %convolution_convert_fusion = bf16[2048,1024]{0,1:T(8,128)(2,1)S(1)} fusion(bf16[512,1024]{1,0:T(8,128)(2,1)} %param.20, bf16[1,1,2048,512]{3,2,1,0:T(8,128)(2,1)S(1)} %copy-done), kind=kOutput, calls=%fused_computation.17 | convolution fusion | flops 2149580800 | bytes 7340032 | tf_op jit(solution)/shard_map/dot_general | solution.py:88
  47.9 1.8 %fusion.53 = (bf16[2048,512]{0,1:T(8,128)(2,1)S(1)}, bf16[2048,512]{0,1:T(8,128)(2,1)}) fusion(bf16[2048,1024]{0,1:T(8,128)(2,1)S(1)} %convolution_convert_fusion), kind=kLoop, calls=%fused_computation.77 | loop fusion | bytes 8388608 | tf_op jit(solution)/shard_map/slice | solution.py:89
  49.7 0.3 broadcast_and_fusion
  50.0 3.2 %fusion.3 = (f32[8,256]{1,0:T(8,128)S(1)}, f32[8,256,2048]{2,1,0:T(8,128)S(1)}) fusion(pred[256,2048]{1,0:T(8,128)(4,1)S(1)} %broadcast_and_fusion, bf16[256,8,64]{0,2,1:T(8,128)(2,1)S(1)} %bitcast.84, bf16[2048,8,64]{0,2,1:T(8,128)(2,1)S(1)} %bitcast.81), kind=kOutput, calls=%fused_computation.12 | convolution fusion | flops 549451776 | bytes 19668992 | tf_op jit(solution)/shard_map/while/body/eval_jaxpr/qhd,khd->hqk/dot_general | solution.py:48
  53.2 5.7 %copy-done.1 = f32[8,256,2048]{2,1,0:T(8,128)} copy-done((f32[8,256,2048]{2,1,0:T(8,128)}, f32[8,256,2048]{2,1,0:T(8,128)S(1)}, u32[]{:S(2)}) %copy-start.1) | copy-done | bytes 16777240
  58.9 5.0 %fusion.4 = f32[8,256]{1,0:T(8,128)S(1)} fusion(f32[8,256,2048]{2,1,0:T(8,128)S(1)} %get-tuple-element.250, f32[8,256]{1,0:T(8,128)S(1)} %get-tuple-element.249, pred[256,2048]{1,0:T(8,128)(4,1)S(1)} %broadcast_and_fusion), kind=kLoop, calls=%fused_computation.13 | loop fusion | flops 20969472 | bytes 17317888 | tf_op jit(solution)/shard_map/while/body/eval_jaxpr/reduce_sum | solution.py:54
  63.9 0.1 reshape.129
  63.9 0.7 reshape.151
  64.6 5.5 %all-to-all-start.2 = ((f32[8,1,256]{2,1,0:T(1,128)}), f32[8,1,256]{2,1,0:T(1,128)S(1)}, u32[]{:S(2)}, u32[]{:S(2)}) async-start(f32[8,1,256]{2,1,0:T(1,128)} %reshape.151), calls=%async_computation.2 | async-start | bytes 16384 | tf_op jit(solution)/shard_map/all_to_all | solution.py:110
  70.2 0.7 reshape.149
  70.9 5.8 %all-to-all-done.2 = f32[8,1,256]{2,1,0:T(1,128)S(1)} async-done(((f32[8,1,256]{2,1,0:T(1,128)}), f32[8,1,256]{2,1,0:T(1,128)S(1)}, u32[]{:S(2)}, u32[]{:S(2)}) %all-to-all-start.2) | async-done | bytes 8224 | tf_op jit(solution)/shard_map/all_to_all | solution.py:110
  76.7 3.3 %all-to-all-start.1 = ((f32[8,1,256]{2,1,0:T(1,128)}), f32[8,1,256]{2,1,0:T(1,128)S(1)}, u32[]{:S(2)}, u32[]{:S(2)}) async-start(f32[8,1,256]{2,1,0:T(1,128)} %reshape.149), calls=%async_computation.1 | async-start | bytes 16384 | tf_op jit(solution)/shard_map/all_to_all | solution.py:111
  80.0 9.4 %fusion.10 = f32[256,8,64]{0,2,1:T(8,128)} fusion(bf16[2048,8,64]{0,2,1:T(8,128)(2,1)} %bitcast.82, f32[8,256,2048]{2,1,0:T(8,128)} %copy-done.1, f32[8,256]{1,0:T(8,128)S(1)} %get-tuple-element.249, pred[256,2048]{1,0:T(8,128)(4,1)S(1)} %broadcast_and_fusion), kind=kOutput, calls=%fused_computation.19 | convolution fusion | flops 557842432 | bytes 19931136 | tf_op jit(solution)/shard_map/while/body/eval_jaxpr/hqk,khd->qhd/dot_general | solution.py:55
  89.4 1.5 copy.28
  90.9 1.1 reshape.126
  92.0 5.9 %all-to-all-start = ((f32[8,32,512]{2,1,0:T(8,128)}), f32[8,32,512]{2,1,0:T(8,128)}, u32[]{:S(2)}, u32[]{:S(2)}) async-start(f32[8,32,512]{2,1,0:T(8,128)} %reshape.126), calls=%async_computation | async-start | bytes 1048576 | tf_op jit(solution)/shard_map/all_to_all | solution.py:109
  98.0 0.6 broadcast.93
  98.5 0.7 reduce.4
  99.3 0.1 reshape.152
  99.3 0.7 reduce.3
  100.1 0.1 reshape.150
  100.2 0.1 copy.31
  100.3 0.3 broadcast_in_dim.86
  100.6 1.1 reshape.128
  101.7 5.2 %all-gather.3 = f32[4,32,8]{1,2,0:T(8,128)S(1)} all-gather(f32[1,32,8]{1,2,0:T(8,128)S(1)} %bitcast.90), channel_id=3, replica_groups=mesh['region'=8,'tm'=4] {'tm'}, dimensions={0}, use_global_device_ids=true | all-gather | bytes 5120 | tf_op jit(solution)/shard_map/all_gather | solution.py:13
  106.9 0.1 copy.34
  107.0 5.2 %all-gather.4 = f32[4,32,8]{1,2,0:T(8,128)S(1)} all-gather(f32[1,32,8]{1,2,0:T(8,128)S(1)} %bitcast.88), channel_id=4, replica_groups=mesh['region'=8,'tm'=4] {'tm'}, dimensions={0}, use_global_device_ids=true | all-gather | bytes 5120 | tf_op jit(solution)/shard_map/all_gather | solution.py:13
  112.2 0.1 copy.35
  112.2 1.3 multiply_reduce_fusion
  113.5 5.8 %all-gather = f32[128,512]{1,0:T(8,128)S(1)} all-gather(f32[32,512]{1,0:T(8,128)S(1)} %multiply_reduce_fusion), channel_id=2, replica_groups=mesh['region'=8,'tm'=4] {'tm'}, dimensions={0}, use_global_device_ids=true | all-gather | bytes 327680 | tf_op jit(solution)/shard_map/all_gather | solution.py:13
  119.4 1.9 %while.12 = (s32[]{:T(128)}, f32[32,512]{1,0:T(8,128)S(1)}, f32[32,8]{1,0:T(8,128)S(1)}, f32[32,8]{1,0:T(8,128)S(1)}, f32[4,32,8]{1,2,0:T(8,128)S(1)}, /*index=5...) while((s32[]{:T(128)}, f32[32,512]{1,0:T(8,128)S(1)}, ...), condition=%wide.region_8.9_spmd, body=%wide.region_7.8_spmd.sunk | while | flops 50693 | bytes 739479 | solution.py:19
  119.4 0.1 copy.48
  119.5 0.1 copy.49
  119.6 0.1 broadcast_in_dim.111
  119.7 0.1 reshape.155
  119.8 0.1 broadcast_in_dim.112
  119.9 0.1 reshape.156
  120.0 0.1 copy.48
  120.1 0.1 copy.49
  120.2 0.1 broadcast_in_dim.111
  120.3 0.1 reshape.155
  120.4 0.1 broadcast_in_dim.112
  120.5 0.1 reshape.156
  120.7 0.1 copy.48
  120.7 0.1 copy.49
  120.8 0.1 broadcast_in_dim.111
  120.9 0.1 reshape.155
  121.0 0.1 broadcast_in_dim.112
  121.1 0.1 reshape.156
  121.3 0.1 broadcast_in_dim.88
  121.4 0.1 reshape.130
  121.5 1.3 fusion.54
  122.8 0.2 multiply_reduce_fusion.1
  123.0 2.2 %fusion.28 = f32[32,512]{1,0:T(8,128)} fusion(bf16[512,512]{1,0:T(8,128)(2,1)} %param.23, bf16[512,512]{1,0:T(8,128)(2,1)} %param.22, f32[32,512]{1,0:T(8,128)S(1)} %get-tuple-element.252, f32[512]{0:T(512)S(1)} %copy-done.3, f32[32]{0:T(128)S(1)} %add_rsqrt_fusion, f32[32]{0:T(128)S(1)} %broadcast_multiply_fusion), kind=kOutput, calls=%fused_computation.46 | convolution fusion | flops 33767424 | bytes 1181952 | tf_op jit(solution)/shard_map/dot_general | solution.py:124
  125.3 33.1 %all-reduce.2.cloned.1.call-done = f32[32,512]{1,0:T(8,128)} async-done(((f32[32,512]{1,0:T(8,128)}), f32[32,512]{1,0:T(8,128)}) %all-reduce.2.cloned.1.call-update) | async-done | bytes 65552 | tf_op jit(solution)/shard_map/psum | solution.py:125
  158.4 1.5 fusion.29
  (34 shorter events, 0.4 us)
Async XLA Ops:
  6.5 37.7 %copy-start = (bf16[1,1,2048,512]{3,2,1,0:T(8,128)(2,1)S(1)}, bf16[1,1,2048,512]{3,2,1,0:T(8,128)(2,1)}, u32[]{:S(2)}) copy-start(bf16[1,1,2048,512]{3,2,1,0:T(8,128)(2,1)} %param.13) | copy-start | bytes 6291460
  53.2 5.7 %copy-start.1 = (f32[8,256,2048]{2,1,0:T(8,128)}, f32[8,256,2048]{2,1,0:T(8,128)S(1)}, u32[]{:S(2)}) copy-start(f32[8,256,2048]{2,1,0:T(8,128)S(1)} %get-tuple-element.250) | copy-start | bytes 50331652
  64.6 12.0 %all-to-all-start.2 = ((f32[8,1,256]{2,1,0:T(1,128)}), f32[8,1,256]{2,1,0:T(1,128)S(1)}, u32[]{:S(2)}, u32[]{:S(2)}) async-start(f32[8,1,256]{2,1,0:T(1,128)} %reshape.151), calls=%async_computation.2 | async-start | bytes 16384 | tf_op jit(solution)/shard_map/all_to_all | solution.py:110
  76.7 15.3 %all-to-all-start.1 = ((f32[8,1,256]{2,1,0:T(1,128)}), f32[8,1,256]{2,1,0:T(1,128)S(1)}, u32[]{:S(2)}, u32[]{:S(2)}) async-start(f32[8,1,256]{2,1,0:T(1,128)} %reshape.149), calls=%async_computation.1 | async-start | bytes 16384 | tf_op jit(solution)/shard_map/all_to_all | solution.py:111
  80.0 41.5 %copy-start.2 = (bf16[1,32,512]{2,1,0:T(8,128)(2,1)S(1)}, bf16[1,32,512]{2,1,0:T(8,128)(2,1)}, u32[]{:S(2)}) copy-start(bf16[1,32,512]{2,1,0:T(8,128)(2,1)} %param.16) | copy-start | bytes 98308
  80.0 43.0 %copy-start.3 = (f32[512]{0:T(512)S(1)}, f32[512]{0:T(512)}, u32[]{:S(2)}) copy-start(f32[512]{0:T(512)} %param.18) | copy-start | bytes 6148
  92.0 20.3 %all-to-all-start = ((f32[8,32,512]{2,1,0:T(8,128)}), f32[8,32,512]{2,1,0:T(8,128)}, u32[]{:S(2)}, u32[]{:S(2)}) async-start(f32[8,32,512]{2,1,0:T(8,128)} %reshape.126), calls=%async_computation | async-start | bytes 1048576 | tf_op jit(solution)/shard_map/all_to_all | solution.py:109
  97.9 60.5 %all-reduce.2.cloned.1.call-start = ((), (), s32[]{:S(2)}) async-start(), calls=%async_computation.3 | async-start | bytes 131072 | tf_op jit(solution)/shard_map/psum | solution.py:125
Sparse Core Ops, SparseCore 0:
  125.4 32.9 all-reduce.1
where the time goes:
time: 167 us
  blocking collectives  48.8 us (29%)
  waiting for transfers between devices  38.9 us (23%)
  matrix products  21.1 us (13%)
  local copies, waits for them, and re-layouts  16.1 us (10%)
  starting transfers between devices  14.8 us (9%)
  between operations  14.2 us (9%)
  other arithmetic  12.7 us (8%)
    psum x1, waiting for transfers between devices, on_device(): mlp_total = lax.psum(mlp_part, 'tm')  33.1 us
    all_gather x1, blocking collectives, on_device(): every_query = lax.all_gather(own_queries, 'region', axis=0, tiled=True)  32.6 us
    all_gather x3, blocking collectives, joined(): everything = jax.tree.map(lambda part: lax.all_gather(part, axis), x)  16.2 us
    dot_general x1, matrix products, partials(): jnp.einsum('hqk,khd->qhd', weights.astype(jnp.bfloat16), value_heads, pre...  9.39 us
    unnamed x12, local copies, waits for them, and re-layouts  7.23 us
    all_to_all x1, starting transfers between devices, on_device(): lax.all_to_all(numerators, 'region', split_axis=0, concat_axis=0, tiled=T...  5.93 us
    all_to_all x1, waiting for transfers between devices, on_device(): lax.all_to_all(denominators, 'region', split_axis=0, concat_axis=0, tiled...  5.75 us
    all_to_all x1, starting transfers between devices, on_device(): lax.all_to_all(denominators, 'region', split_axis=0, concat_axis=0, tiled...  5.52 us
  transfers between devices with their start and end apart: 4, of which 2 were waited for; matrix products, arithmetic and copies ran while one was open for 10% of the time, Pallas kernels for 0%

commit v1 on v0

--- a/solution.py
+++ b/solution.py
@@ -122,7 +122,7 @@
         jnp.dot(normed2, w_up, preferred_element_type=jnp.float32), approximate=True
     ).astype(jnp.bfloat16)
     mlp_part = jnp.dot(hidden, w_down, preferred_element_type=jnp.float32)
-    mlp_total = lax.psum(mlp_part, "tm")
+    mlp_total = jnp.sum(lax.all_gather(mlp_part, "tm"), axis=0)
     return (residual + mlp_total).astype(jnp.bfloat16)[None]
 
 

time: 167 us -> 125 us (0.75)
  waiting for transfers between devices: 38.9 us -> 5.76 us
  between operations: 14.2 us -> 0.86 us
  blocking collectives: 48.8 us -> 54.6 us
    psum x1 -> x0, waiting for transfers between devices: 33.1 us -> none  [on_device(): mlp_total = lax.psum(mlp_part, 'tm')]
    all_gather x0 -> x1, blocking collectives: none -> 5.85 us  [on_device(): mlp_total = jnp.sum(lax.all_gather(mlp_part, 'tm'), axis=0)]
  transfers between devices with their start and end apart: 4 -> 3, of which waited for: 2 -> 1; matrix products, arithmetic and copies ran while one was open for 10% -> 13% of each run, Pallas kernels for 0% -> 0%
where the time goes in v1:
time: 125 us
  blocking collectives  54.6 us (44%)
  matrix products  20.4 us (16%)
  local copies, waits for them, and re-layouts  16.1 us (13%)
  starting transfers between devices  14.8 us (12%)
  other arithmetic  11.9 us (10%)
  waiting for transfers between devices  5.76 us (5%)
    all_gather x1, blocking collectives, on_device(): every_query = lax.all_gather(own_queries, 'region', axis=0, tiled=True)  32.6 us
    all_gather x3, blocking collectives, joined(): everything = jax.tree.map(lambda part: lax.all_gather(part, axis), x)  16.2 us
    dot_general x1, matrix products, partials(): jnp.einsum('hqk,khd->qhd', weights.astype(jnp.bfloat16), value_heads, pre...  9.39 us
    unnamed x12, local copies, waits for them, and re-layouts  7.23 us
    all_to_all x1, starting transfers between devices, on_device(): lax.all_to_all(numerators, 'region', split_axis=0, concat_axis=0, tiled=T...  5.93 us
    all_gather x1, blocking collectives, on_device(): mlp_total = jnp.sum(lax.all_gather(mlp_part, 'tm'), axis=0)  5.85 us
    all_to_all x1, waiting for transfers between devices, on_device(): lax.all_to_all(denominators, 'region', split_axis=0, concat_axis=0, tiled...  5.75 us
    all_to_all x1, starting transfers between devices, on_device(): lax.all_to_all(denominators, 'region', split_axis=0, concat_axis=0, tiled...  5.52 us
  transfers between devices with their start and end apart: 3, of which 1 were waited for; matrix products, arithmetic and copies ran while one was open for 13% of the time, Pallas kernels for 0%

profile of v1, /device:TPU:0, one launch (start us, length us, event | category | flops | bytes accessed | tf_op | source)
XLA Modules:
  0.0 124.6 jit_solution(2754602983105251853)
XLA Ops:
  0.0 1.0 fusion.44
  1.0 0.1 broadcast_in_dim.82
  1.1 0.1 and.27
  1.9 0.9 convert_reduce_fusion
  2.7 0.9 fusion.16
  3.7 1.3 %convolution_convert_fusion.1 = bf16[32,512]{1,0:T(8,128)(2,1)S(1)} fusion(bf16[512,512]{1,0:T(8,128)(2,1)} %param.19, bf16[1,32,512]{2,1,0:T(8,128)(2,1)} %param.16, f32[512]{0:T(512)} %param.17, f32[32]{0:T(128)S(1)} %add_rsqrt_fusion.1, f32[32]{0:T(128)S(1)} %broadcast_multiply_fusion.1), kind=kOutput, calls=%fused_computation.21 | convolution fusion | flops 16875520 | bytes 592128 | tf_op jit(solution)/shard_map/dot_general | solution.py:86
  5.0 32.6 %all_gather.25 = bf16[256,512]{1,0:T(8,128)(2,1)S(1)} all-gather(bf16[32,512]{1,0:T(8,128)(2,1)S(1)} %convolution_convert_fusion.1), channel_id=1, replica_groups=mesh['region'=8,'tm'=4] {'region'}, dimensions={0}, use_global_device_ids=true | all-gather | bytes 294912 | tf_op jit(solution)/shard_map/all_gather | solution.py:87
  37.6 0.1 copy.27
  37.7 3.6 %convolution_convert_fusion = bf16[2048,1024]{0,1:T(8,128)(2,1)S(1)} fusion(bf16[512,1024]{1,0:T(8,128)(2,1)} %param.20, bf16[1,1,2048,512]{3,2,1,0:T(8,128)(2,1)S(1)} %copy-done), kind=kOutput, calls=%fused_computation.17 | convolution fusion | flops 2149580800 | bytes 7340032 | tf_op jit(solution)/shard_map/dot_general | solution.py:88
  41.3 1.8 %fusion.53 = (bf16[2048,512]{0,1:T(8,128)(2,1)S(1)}, bf16[2048,512]{0,1:T(8,128)(2,1)}) fusion(bf16[2048,1024]{0,1:T(8,128)(2,1)S(1)} %convolution_convert_fusion), kind=kLoop, calls=%fused_computation.77 | loop fusion | bytes 8388608 | tf_op jit(solution)/shard_map/slice | solution.py:89
  43.1 0.3 broadcast_and_fusion
  43.4 3.2 %fusion.3 = (f32[8,256]{1,0:T(8,128)S(1)}, f32[8,256,2048]{2,1,0:T(8,128)S(1)}) fusion(pred[256,2048]{1,0:T(8,128)(4,1)S(1)} %broadcast_and_fusion, bf16[256,8,64]{0,2,1:T(8,128)(2,1)S(1)} %bitcast.85, bf16[2048,8,64]{0,2,1:T(8,128)(2,1)S(1)} %bitcast.82), kind=kOutput, calls=%fused_computation.12 | convolution fusion | flops 549451776 | bytes 19668992 | tf_op jit(solution)/shard_map/while/body/eval_jaxpr/qhd,khd->hqk/dot_general | solution.py:48
  46.6 5.7 %copy-done.1 = f32[8,256,2048]{2,1,0:T(8,128)} copy-done((f32[8,256,2048]{2,1,0:T(8,128)}, f32[8,256,2048]{2,1,0:T(8,128)S(1)}, u32[]{:S(2)}) %copy-start.1) | copy-done | bytes 16777240
  52.4 5.0 %fusion.4 = f32[8,256]{1,0:T(8,128)S(1)} fusion(f32[8,256,2048]{2,1,0:T(8,128)S(1)} %get-tuple-element.250, f32[8,256]{1,0:T(8,128)S(1)} %get-tuple-element.249, pred[256,2048]{1,0:T(8,128)(4,1)S(1)} %broadcast_and_fusion), kind=kLoop, calls=%fused_computation.13 | loop fusion | flops 20969472 | bytes 17317888 | tf_op jit(solution)/shard_map/while/body/eval_jaxpr/reduce_sum | solution.py:54
  57.3 0.1 reshape.129
  57.4 0.7 reshape.152
  58.1 5.5 %all-to-all-start.2 = ((f32[8,1,256]{2,1,0:T(1,128)}), f32[8,1,256]{2,1,0:T(1,128)S(1)}, u32[]{:S(2)}, u32[]{:S(2)}) async-start(f32[8,1,256]{2,1,0:T(1,128)} %reshape.152), calls=%async_computation.2 | async-start | bytes 16384 | tf_op jit(solution)/shard_map/all_to_all | solution.py:110
  63.7 0.7 reshape.150
  64.4 5.8 %all-to-all-done.2 = f32[8,1,256]{2,1,0:T(1,128)S(1)} async-done(((f32[8,1,256]{2,1,0:T(1,128)}), f32[8,1,256]{2,1,0:T(1,128)S(1)}, u32[]{:S(2)}, u32[]{:S(2)}) %all-to-all-start.2) | async-done | bytes 8224 | tf_op jit(solution)/shard_map/all_to_all | solution.py:110
  70.1 3.3 %all-to-all-start.1 = ((f32[8,1,256]{2,1,0:T(1,128)}), f32[8,1,256]{2,1,0:T(1,128)S(1)}, u32[]{:S(2)}, u32[]{:S(2)}) async-start(f32[8,1,256]{2,1,0:T(1,128)} %reshape.150), calls=%async_computation.1 | async-start | bytes 16384 | tf_op jit(solution)/shard_map/all_to_all | solution.py:111
  73.5 9.4 %fusion.10 = f32[256,8,64]{0,2,1:T(8,128)} fusion(bf16[2048,8,64]{0,2,1:T(8,128)(2,1)} %bitcast.83, f32[8,256,2048]{2,1,0:T(8,128)} %copy-done.1, f32[8,256]{1,0:T(8,128)S(1)} %get-tuple-element.249, pred[256,2048]{1,0:T(8,128)(4,1)S(1)} %broadcast_and_fusion), kind=kOutput, calls=%fused_computation.19 | convolution fusion | flops 557842432 | bytes 19931136 | tf_op jit(solution)/shard_map/while/body/eval_jaxpr/hqk,khd->qhd/dot_general | solution.py:55
  82.9 1.5 %copy.28 = f32[256,8,64]{2,1,0:T(8,128)S(1)} copy(f32[256,8,64]{0,2,1:T(8,128)} %fusion.10) | data formatting | bytes 1048576 | tf_op jit(solution)/shard_map/while/body/eval_jaxpr/hqk,khd->qhd/transpose | solution.py:55
  84.4 1.1 reshape.126
  85.5 5.9 %all-to-all-start = ((f32[8,32,512]{2,1,0:T(8,128)}), f32[8,32,512]{2,1,0:T(8,128)}, u32[]{:S(2)}, u32[]{:S(2)}) async-start(f32[8,32,512]{2,1,0:T(8,128)} %reshape.126), calls=%async_computation | async-start | bytes 1048576 | tf_op jit(solution)/shard_map/all_to_all | solution.py:109
  91.4 0.6 broadcast.93
  92.0 0.7 reduce.4
  92.7 0.1 reshape.153
  92.8 0.7 reduce.3
  93.5 0.1 reshape.151
  93.6 0.1 copy.31
  93.7 0.3 broadcast_in_dim.86
  94.0 1.1 reshape.128
  95.1 5.2 %all-gather.4 = f32[4,32,8]{1,2,0:T(8,128)S(1)} all-gather(f32[1,32,8]{1,2,0:T(8,128)S(1)} %bitcast.92), channel_id=3, replica_groups=mesh['region'=8,'tm'=4] {'tm'}, dimensions={0}, use_global_device_ids=true | all-gather | bytes 5120 | tf_op jit(solution)/shard_map/all_gather | solution.py:13
  100.3 0.1 copy.34
  100.4 5.2 %all-gather.5 = f32[4,32,8]{1,2,0:T(8,128)S(1)} all-gather(f32[1,32,8]{1,2,0:T(8,128)S(1)} %bitcast.90), channel_id=4, replica_groups=mesh['region'=8,'tm'=4] {'tm'}, dimensions={0}, use_global_device_ids=true | all-gather | bytes 5120 | tf_op jit(solution)/shard_map/all_gather | solution.py:13
  105.6 0.1 copy.35
  105.7 1.3 %multiply_reduce_fusion = f32[32,512]{1,0:T(8,128)S(1)} fusion(f32[8,32,512]{2,1,0:T(8,128)} %all-to-all-done, f32[8,32,512]{2,1,0:T(8,128)} %reshape.128), kind=kLoop, calls=%fused_computation.23 | loop fusion | flops 245760 | bytes 1114112 | tf_op jit(solution)/shard_map/reduce_sum | solution.py:115
  106.9 5.8 %all-gather = f32[128,512]{1,0:T(8,128)S(1)} all-gather(f32[32,512]{1,0:T(8,128)S(1)} %multiply_reduce_fusion), channel_id=2, replica_groups=mesh['region'=8,'tm'=4] {'tm'}, dimensions={0}, use_global_device_ids=true | all-gather | bytes 327680 | tf_op jit(solution)/shard_map/all_gather | solution.py:13
  112.8 1.9 %while.12 = (s32[]{:T(128)}, f32[32,512]{1,0:T(8,128)S(1)}, f32[32,8]{1,0:T(8,128)S(1)}, f32[32,8]{1,0:T(8,128)S(1)}, f32[4,32,8]{1,2,0:T(8,128)S(1)}, /*index=5...) while((s32[]{:T(128)}, f32[32,512]{1,0:T(8,128)S(1)}, ...), condition=%wide.region_8.9_spmd, body=%wide.region_7.8_spmd.sunk | while | flops 50693 | bytes 739479 | solution.py:19
  112.8 0.1 copy.48
  112.9 0.1 copy.49
  113.0 0.1 broadcast_in_dim.111
  113.1 0.1 reshape.156
  113.2 0.1 broadcast_in_dim.112
  113.3 0.1 reshape.157
  113.4 0.1 copy.48
  113.5 0.1 copy.49
  113.6 0.1 broadcast_in_dim.111
  113.7 0.1 reshape.156
  113.8 0.1 broadcast_in_dim.112
  113.9 0.1 reshape.157
  114.1 0.1 copy.48
  114.2 0.1 copy.49
  114.3 0.1 broadcast_in_dim.111
  114.4 0.1 reshape.156
  114.5 0.1 broadcast_in_dim.112
  114.6 0.1 reshape.157
  114.7 0.1 broadcast_in_dim.88
  114.8 0.1 reshape.130
  114.9 1.3 %fusion.54 = (f32[32]{0:T(128)S(1)}, f32[32,512]{1,0:T(8,128)S(1)}) fusion(bf16[512,512]{1,0:T(8,128)(2,1)} %param.21, f32[32,512]{1,0:T(8,128)S(1)} %get-tuple-element.209, f32[32,512]{1,0:T(8,128)S(1)} %reshape.130, bf16[1,32,512]{2,1,0:T(8,128)(2,1)S(1)} %copy-done.2), kind=kOutput, calls=%fused_computation.78 | convolution fusion | flops 16859104 | bytes 753792 | tf_op jit(solution)/shard_map/dot_general | solution.py:119
  116.3 0.2 multiply_reduce_fusion.1
  116.5 1.6 %fusion.28 = f32[32,512]{1,0:T(8,128)S(1)} fusion(bf16[512,512]{1,0:T(8,128)(2,1)} %param.23, bf16[512,512]{1,0:T(8,128)(2,1)} %param.22, f32[32,512]{1,0:T(8,128)S(1)} %get-tuple-element.252, f32[512]{0:T(512)S(1)} %copy-done.3, f32[32]{0:T(128)S(1)} %add_rsqrt_fusion, f32[32]{0:T(128)S(1)} %broadcast_multiply_fusion), kind=kOutput, calls=%fused_computation.46 | convolution fusion | flops 33767424 | bytes 1181952 | tf_op jit(solution)/shard_map/dot_general | solution.py:124
  118.1 5.9 %all-gather.3 = f32[128,512]{1,0:T(8,128)S(1)} all-gather(f32[32,512]{1,0:T(8,128)S(1)} %fusion.28), channel_id=5, replica_groups=mesh['region'=8,'tm'=4] {'tm'}, dimensions={0}, use_global_device_ids=true | all-gather | bytes 327680 | tf_op jit(solution)/shard_map/all_gather | solution.py:125
  123.9 0.6 fusion.29
  (33 shorter events, 0.4 us)
Async XLA Ops:
  0.0 37.7 %copy-start = (bf16[1,1,2048,512]{3,2,1,0:T(8,128)(2,1)S(1)}, bf16[1,1,2048,512]{3,2,1,0:T(8,128)(2,1)}, u32[]{:S(2)}) copy-start(bf16[1,1,2048,512]{3,2,1,0:T(8,128)(2,1)} %param.13) | copy-start | bytes 6291460
  46.6 5.7 %copy-start.1 = (f32[8,256,2048]{2,1,0:T(8,128)}, f32[8,256,2048]{2,1,0:T(8,128)S(1)}, u32[]{:S(2)}) copy-start(f32[8,256,2048]{2,1,0:T(8,128)S(1)} %get-tuple-element.250) | copy-start | bytes 50331652
  58.1 12.0 %all-to-all-start.2 = ((f32[8,1,256]{2,1,0:T(1,128)}), f32[8,1,256]{2,1,0:T(1,128)S(1)}, u32[]{:S(2)}, u32[]{:S(2)}) async-start(f32[8,1,256]{2,1,0:T(1,128)} %reshape.152), calls=%async_computation.2 | async-start | bytes 16384 | tf_op jit(solution)/shard_map/all_to_all | solution.py:110
  70.1 15.3 %all-to-all-start.1 = ((f32[8,1,256]{2,1,0:T(1,128)}), f32[8,1,256]{2,1,0:T(1,128)S(1)}, u32[]{:S(2)}, u32[]{:S(2)}) async-start(f32[8,1,256]{2,1,0:T(1,128)} %reshape.150), calls=%async_computation.1 | async-start | bytes 16384 | tf_op jit(solution)/shard_map/all_to_all | solution.py:111
  73.5 41.4 %copy-start.2 = (bf16[1,32,512]{2,1,0:T(8,128)(2,1)S(1)}, bf16[1,32,512]{2,1,0:T(8,128)(2,1)}, u32[]{:S(2)}) copy-start(bf16[1,32,512]{2,1,0:T(8,128)(2,1)} %param.16) | copy-start | bytes 98308
  73.5 43.0 %copy-start.3 = (f32[512]{0:T(512)S(1)}, f32[512]{0:T(512)}, u32[]{:S(2)}) copy-start(f32[512]{0:T(512)} %param.18) | copy-start | bytes 6148
  85.5 20.2 %all-to-all-start = ((f32[8,32,512]{2,1,0:T(8,128)}), f32[8,32,512]{2,1,0:T(8,128)}, u32[]{:S(2)}, u32[]{:S(2)}) async-start(f32[8,32,512]{2,1,0:T(8,128)} %reshape.126), calls=%async_computation | async-start | bytes 1048576 | tf_op jit(solution)/shard_map/all_to_all | solution.py:109
